TPU v7x, 32 devices: a whole 2x2x4 slice. The times are simulated.
32 devices in a mesh: prow: 8 (over z, core), pcol: 4 (over y, x).
Axes of the slice: x: 2, y: 2, z: 4, core: 2. Of those that a mesh axis runs over, the one named last changes fastest.
Arguments:
- matrix: float32 [8192, 24576], P('prow', 'pcol'), may hold values from -14 to 104.50967, as said below
Outputs:
- factored: float32 [8192, 24576], P('prow', 'pcol')
- tfactors: float32 [2, 128, 128], replicated
Inputs may be any that keep to these rules, and one draw needn't show every extreme that they name: `matrix`: real entries.
All inputs are finite; a program needn't handle non-finite values.
Results may differ from a plain program's by a relative error of at most 0.0003.
Values sent between devices are 32-bit elements; how exact they have to be, the bound alone decides.
A program may use at most 192 MiB of HBM per device.

v0:
```python
import jax
import jax.numpy as jnp
from jax import lax
from jax.sharding import PartitionSpec as P

NB = 128


highest = lax.Precision.HIGHEST


def broadcast(value, axis, root):
    mine = lax.axis_index(axis) == root
    return lax.psum(jnp.where(mine, value, jnp.zeros_like(value)), axis)


def transposed_product(left, right):
    return lax.dot_general(
        left, right, (((0,), (0,)), ((), ())), precision=highest, preferred_element_type=jnp.float32
    )


def matmul(left, right):
    return jnp.dot(left, right, precision=highest, preferred_element_type=jnp.float32)


def unit_inverse(strict_part):
    size_now = strict_part.shape[0]
    identity = jnp.eye(size_now, dtype=jnp.float32)
    term = identity
    total = identity
    for power in range(size_now - 1):
        term = -matmul(term, strict_part)
        total = total + term
    return total


def cholesky_pair(square):
    block_size = square.shape[0]
    if block_size <= 8:
        row_ids = jnp.arange(block_size)
        lower_part = jnp.zeros((block_size, block_size), jnp.float32)
        working = square
        for column in range(block_size):
            pivot = jnp.sqrt(working[column, column])
            column_values = jnp.where(row_ids >= column, working[:, column] / pivot, 0.0)
            lower_part = (
                lower_part
                + column_values[:, None] * (row_ids == column).astype(jnp.float32)[None, :]
            )
            working = working - column_values[:, None] * column_values[None, :]
        diagonal_values = jnp.diagonal(lower_part)
        unit_part = lower_part / diagonal_values[None, :]
        identity = jnp.eye(block_size, dtype=jnp.float32)
        lower_inverse = unit_inverse(unit_part - identity) / diagonal_values[:, None]
        return (lower_part, lower_inverse)
    middle = block_size // 2
    top_lower, top_inverse = cholesky_pair(square[:middle, :middle])
    left_lower = matmul(square[middle:, :middle], top_inverse.T)
    rest_lower, rest_inverse = cholesky_pair(
        square[middle:, middle:] - matmul(left_lower, left_lower.T)
    )
    zero_block = jnp.zeros((middle, block_size - middle), jnp.float32)
    lower_part = jnp.block([[top_lower, zero_block], [left_lower, rest_lower]])
    corner_inverse = -matmul(rest_inverse, matmul(left_lower, top_inverse))
    lower_inverse = jnp.block([[top_inverse, zero_block], [corner_inverse, rest_inverse]])
    return (lower_part, lower_inverse)


def lower_upper(square):
    block_size = square.shape[0]
    identity = jnp.eye(block_size, dtype=jnp.float32)
    if block_size <= 8:
        row_ids = jnp.arange(block_size)
        lower_part = identity
        working = square
        for column in range(block_size):
            multipliers = jnp.where(
                row_ids > column, working[:, column] / working[column, column], 0.0
            )
            lower_part = (
                lower_part + multipliers[:, None] * (row_ids == column).astype(jnp.float32)[None, :]
            )
            working = working - multipliers[:, None] * working[column, :][None, :]
        upper_part = jnp.triu(working)
        lower_inverse = unit_inverse(lower_part - identity)
        diagonal_values = jnp.diagonal(upper_part)
        upper_inverse = (
            unit_inverse(upper_part / diagonal_values[:, None] - identity)
            / diagonal_values[None, :]
        )
        return (lower_part, lower_inverse, upper_part, upper_inverse)
    middle = block_size // 2
    top_lower, top_lower_inv, top_upper, top_upper_inv = lower_upper(square[:middle, :middle])
    right_upper = matmul(top_lower_inv, square[:middle, middle:])
    left_lower = matmul(square[middle:, :middle], top_upper_inv)
    rest_lower, rest_lower_inv, rest_upper, rest_upper_inv = lower_upper(
        square[middle:, middle:] - matmul(left_lower, right_upper)
    )
    zero_block = jnp.zeros((middle, block_size - middle), jnp.float32)
    lower_part = jnp.block([[top_lower, zero_block], [left_lower, rest_lower]])
    upper_part = jnp.block([[top_upper, right_upper], [zero_block.T, rest_upper]])
    lower_corner = -matmul(rest_lower_inv, matmul(left_lower, top_lower_inv))
    upper_corner = -matmul(top_upper_inv, matmul(right_upper, rest_upper_inv))
    lower_inverse = jnp.block([[top_lower_inv, zero_block], [lower_corner, rest_lower_inv]])
    upper_inverse = jnp.block([[top_upper_inv, upper_corner], [zero_block.T, rest_upper_inv]])
    return (lower_part, lower_inverse, upper_part, upper_inverse)


def factor_panel(panel_cols, first_row, global_rows, my_row):
    rows_dev = panel_cols.shape[0]
    offset = first_row % rows_dev
    is_owner = my_row == first_row // rows_dev
    masked = jnp.where((global_rows >= first_row)[:, None], panel_cols, 0.0)
    corner = jnp.where(is_owner, panel_cols[offset : offset + NB], 0.0)
    gram_matrix, top_block = lax.psum((transposed_product(masked, masked), corner), "prow")
    identity = jnp.eye(NB, dtype=jnp.float32)
    chol_lower, chol_inverse = cholesky_pair(gram_matrix)
    upper_inverse = chol_inverse.T
    square = identity + matmul(top_block, upper_inverse)
    unit_lower, lower_inverse, wy_upper, wy_inverse = lower_upper(square)
    reflectors = matmul(masked, matmul(upper_inverse, wy_inverse))
    patched = reflectors.at[offset : offset + NB].add(wy_inverse)
    reflectors = jnp.where(is_owner, patched, reflectors)
    tfactor = matmul(wy_upper, lower_inverse.T)
    corner_packed = jnp.triu(-chol_lower.T) + jnp.tril(unit_lower, -1)
    packed_panel = jnp.where((global_rows < first_row)[:, None], panel_cols, reflectors)
    packed_panel = jnp.where(
        is_owner, packed_panel.at[offset : offset + NB].set(corner_packed), packed_panel
    )
    return (reflectors, tfactor, packed_panel)


def per_device(matrix):
    rows_dev, cols_dev = matrix.shape
    my_row = lax.axis_index("prow")
    my_col = lax.axis_index("pcol")
    global_rows = my_row * rows_dev + jnp.arange(rows_dev, dtype=jnp.int32)
    own_cols = my_col * cols_dev + jnp.arange(cols_dev, dtype=jnp.int32)
    owned = matrix
    panels = broadcast(matrix[:, : 2 * NB], "pcol", 0)
    factors = []
    packed_results = []
    for panel_index in range(2):
        first_row = panel_index * NB
        source = panels[:, first_row : first_row + NB]
        reflectors, tfactor, packed_panel = factor_panel(source, first_row, global_rows, my_row)
        if panel_index == 0:
            target = jnp.concatenate([panels[:, NB : 2 * NB], owned], axis=1)
            target_ids = jnp.concatenate([NB + jnp.arange(NB, dtype=jnp.int32), own_cols])
        else:
            target = owned
            target_ids = own_cols
        products = lax.psum(transposed_product(reflectors, target), "prow")
        update = matmul(reflectors, matmul(tfactor.T, products))
        target = jnp.where((target_ids >= first_row + NB)[None, :], target - update, target)
        if panel_index == 0:
            panels = jnp.concatenate([panels[:, :NB], target[:, :NB]], axis=1)
            owned = target[:, NB:]
        else:
            owned = target
        factors.append(tfactor)
        packed_results.append(packed_panel)
    first_t, second_t = factors
    leading_packed_panel, following_packed_panel = packed_results
    packed_both = jnp.concatenate([leading_packed_panel, following_packed_panel], axis=1)
    result = owned.at[:, : 2 * NB].set(jnp.where(my_col == 0, packed_both, owned[:, : 2 * NB]))
    return (result, jnp.stack([first_t, second_t]))


def solution(mesh):
    placed = (P("prow", "pcol"),)
    return jax.shard_map(
        per_device, mesh=mesh, in_specs=placed, out_specs=(P("prow", "pcol"), P()), check_vma=False
    )
```

profile of v0, /device:TPU:0, one launch (start us, length us, event | category | flops | bytes accessed | tf_op | source)
XLA Modules:
  0.0 1456.2 jit_solution(11789288657180956184)
XLA Ops:
  7.2 1.3 slice.4711
  8.9 1.0 broadcast_select_fusion
  14.2 52.6 %all-reduce.188.cloned.1.call-done = f32[1024,256]{0,1:T(8,128)} async-done(((f32[1024,256]{0,1:T(8,128)}), f32[1024,256]{0,1:T(8,128)}) %all-reduce.188.cloned.1.call-update) | async-done | bytes 1048592 | tf_op jit(solution)/shard_map/psum | solution.py:14
  66.8 1.6 slice_select_fusion.5
  68.4 2.4 fusion.169
  71.5 54.6 %all-reduce.196.cloned.1.call-done = (f32[128,128]{1,0:T(8,128)}, f32[128,128]{0,1:T(8,128)}) async-done(((f32[128,128]{1,0:T(8,128)}, f32[128,128]{0,1:T(8,128)}), (f32[128,128]{1,0:T(8,128)}, f32[128,128]{0,1:T(8,128)})) %all-reduce.196.cloned.1.call-update) | async-done | bytes 131088 | tf_op jit(solution)/shard_map/psum | solution.py:116
  126.1 1.2 slice.6316
  128.0 0.8 fusion.1096
  142.1 0.8 multiply_subtract_fusion.410
  146.0 0.8 fusion.1089
  147.0 0.8 convolution_subtract_fusion.59
  161.9 0.8 fusion.593
  162.9 0.8 convolution_subtract_fusion.27
  192.4 0.9 fusion.470
  193.4 0.9 convolution_subtract_fusion.11
  252.0 1.0 fusion.351
  253.2 0.9 convolution_subtract_fusion.3
  370.2 1.1 convolution_add_fusion.1
  626.5 0.8 slice_select_fusion
  627.5 19.9 %fusion.2 = f32[128,6272]{1,0:T(8,128)} fusion(f32[1024,128]{0,1:T(8,128)S(1)} %fusion.181, f32[1024,6144]{1,0:T(8,128)} %param.11, f32[1024,128]{1,0:T(8,128)S(1)} %copy.1064), kind=kOutput, calls=%fused_computation.69 | convolution fusion | flops 9871425536 | bytes 29425664 | tf_op jit(solution)/shard_map/dot_general | solution.py:18
  652.3 72.5 %all-reduce.190.cloned.1.call-done = f32[128,6272]{1,0:T(8,128)} async-done(((f32[128,6272]{1,0:T(8,128)}), f32[128,6272]{1,0:T(8,128)}) %all-reduce.190.cloned.1.call-update) | async-done | bytes 3211280 | tf_op jit(solution)/shard_map/psum | solution.py:154
  724.7 4.9 fusion.1888
  729.7 26.5 %subtract_select_fusion = f32[1024,6272]{1,0:T(8,128)} fusion(f32[1024,6144]{1,0:T(8,128)} %param.11, f32[1024,128]{1,0:T(8,128)S(1)} %copy.1064, f32[1024,128]{0,1:T(8,128)S(1)} %fusion.181, f32[128,6272]{1,0:T(8,128)S(1)} %fusion.1888, pred[6272]{0:T(1024)(128)(4,1)S(1)} %add_compare_fusion), kind=kOutput, calls=%fused_computation.64 | convolution fusion | flops 9884270592 | bytes 55122048 | tf_op jit(solution)/shard_map/dot_general | solution.py:24
  756.2 1.1 slice.6449
  757.2 1.5 slice_select_fusion.4
  758.9 1.2 fusion.166
  760.8 54.7 %all-reduce.194.cloned.1.call-done = (f32[128,128]{1,0:T(8,128)}, f32[128,128]{1,0:T(8,128)}) async-done(((f32[128,128]{1,0:T(8,128)}, f32[128,128]{1,0:T(8,128)}), (f32[128,128]{1,0:T(8,128)}, f32[128,128]{1,0:T(8,128)})) %all-reduce.194.cloned.1.call-update) | async-done | bytes 131088 | tf_op jit(solution)/shard_map/psum | solution.py:116
  815.5 1.2 slice.6451
  817.4 0.8 fusion.1104
  829.3 0.8 multiply_subtract_fusion.203
  831.5 0.8 multiply_subtract_fusion.202
  835.4 0.8 fusion.1041
  836.3 0.8 convolution_subtract_fusion.43
  851.4 0.8 fusion.569
  852.2 0.8 convolution_subtract_fusion.19
  881.9 0.9 fusion.455
  882.8 0.9 convolution_subtract_fusion.7
  941.6 1.0 fusion.337
  942.6 0.9 convolution_subtract_fusion.1
  994.6 1.0 slice.5664
  1060.2 1.1 convolution_add_fusion
  1310.5 0.8 select_reduce_fusion
  1320.7 18.9 %fusion = f32[128,6144]{1,0:T(8,128)} fusion(f32[1024,128]{1,0:T(8,128)S(1)} %constant_dynamic-update-slice_fusion, f32[1024,6272]{1,0:T(8,128)} %subtract_select_fusion), kind=kOutput, calls=%fused_computation.67 | convolution fusion | flops 9663676416 | bytes 28835840 | tf_op jit(solution)/shard_map/dot_general | solution.py:18
  1343.8 1.3 broadcast_select_fusion.1
  1345.3 70.3 %all-reduce.192.cloned.1.call-done = f32[128,6144]{1,0:T(8,128)} async-done(((f32[128,6144]{1,0:T(8,128)}), f32[128,6144]{1,0:T(8,128)}) %all-reduce.192.cloned.1.call-update) | async-done | bytes 3145744 | tf_op jit(solution)/shard_map/psum | solution.py:154
  1415.6 4.7 fusion.1934
  1420.3 25.9 %subtract_select_fusion.1 = f32[1024,6144]{1,0:T(8,128)} fusion(f32[1024,6272]{1,0:T(8,128)} %subtract_select_fusion, pred[6144]{0:T(1024)(128)(4,1)S(1)} %broadcast_compare_fusion, f32[1024,128]{1,0:T(8,128)S(1)} %constant_dynamic-update-slice_fusion, f32[128,6144]{1,0:T(8,128)S(1)} %fusion.1934), kind=kOutput, calls=%fused_computation.65 | convolution fusion | flops 9676259328 | bytes 54007808 | tf_op jit(solution)/shard_map/dot_general | solution.py:24
  1446.2 3.0 fusion.163
  (3338 shorter events, 813.3 us)
Async XLA Ops:
  7.2 59.6 %all-reduce.188.cloned.1.call-start = ((), (), s32[]{:S(2)}) async-start(), calls=%async_computation | async-start | bytes 2097152 | tf_op jit(solution)/shard_map/psum | solution.py:14
  9.9 116.2 %all-reduce.196.cloned.1.call-start = ((), (), s32[]{:S(2)}) async-start(), calls=%async_computation.4 | async-start | bytes 262144 | tf_op jit(solution)/shard_map/psum | solution.py:116
  10.0 0.6 copy-start.3
  66.8 558.9 %copy-start = (f32[1024,256]{0,1:T(8,128)S(1)}, f32[1024,256]{0,1:T(8,128)}, u32[]{:S(2)}) copy-start(f32[1024,256]{0,1:T(8,128)} %all-reduce.188.cloned.1.call-done) | copy-start | bytes 3145732
  70.8 653.9 %all-reduce.190.cloned.1.call-start = ((), (), s32[]{:S(2)}) async-start(), calls=%async_computation.1 | async-start | bytes 6422528 | tf_op jit(solution)/shard_map/psum | solution.py:154
  647.4 168.0 %all-reduce.194.cloned.1.call-start = ((), (), s32[]{:S(2)}) async-start(), calls=%async_computation.3 | async-start | bytes 262144 | tf_op jit(solution)/shard_map/psum | solution.py:116
  729.6 29.3 %copy-start.2 = (pred[1024]{0:T(1024)(128)(4,1)S(1)}, pred[1024]{0:T(1024)(128)(4,1)}, u32[]{:S(2)}) copy-start(pred[1024]{0:T(1024)(128)(4,1)} %fusion.1094) | copy-start | bytes 3076
  729.7 30.8 %copy-start.4 = (s32[128]{0:T(128)S(1)}, s32[128]{0:T(128)}, u32[]{:S(2)}) copy-start(s32[128]{0:T(128)} %copy-done.3) | copy-start | bytes 1540
  756.2 427.5 %copy-start.1 = (pred[8,8]{1,0:T(8,128)(4,1)S(1)}, pred[8,8]{1,0:T(8,128)(4,1)}, u32[]{:S(2)}) copy-start(pred[8,8]{1,0:T(8,128)(4,1)} %copy.1866) | copy-start | bytes 196
  756.2 554.3 %copy-start.5 = (pred[8,1]{1,0:T(8,128)(4,1)S(1)}, pred[8,1]{1,0:T(8,128)(4,1)}, u32[]{:S(2)}) copy-start(pred[8,1]{1,0:T(8,128)(4,1)} %copy.2036) | copy-start | bytes 28
  760.2 655.4 %all-reduce.192.cloned.1.call-start = ((), (), s32[]{:S(2)}) async-start(), calls=%async_computation.2 | async-start | bytes 6291456 | tf_op jit(solution)/shard_map/psum | solution.py:154
  1185.4 158.5 %copy-start.6 = (pred[1024]{0:T(1024)(128)(4,1)S(1)}, pred[1024]{0:T(1024)(128)(4,1)}, u32[]{:S(2)}) copy-start(pred[1024]{0:T(1024)(128)(4,1)} %fusion.1092) | copy-start | bytes 3076
Sparse Core Ops, SparseCore 0:
  11.6 55.1 all-reduce.187
  70.9 55.1 all-reduce.195
  647.6 77.1 all-reduce.189
  760.3 55.1 all-reduce.193
  1339.7 75.8 all-reduce.191
where the time goes:
time: 1470 us; the launch traced here: 1460 us
  local copies, waits for them, and re-layouts  395 us (27%)
  waiting for transfers between devices  305 us (21%)
  other arithmetic  287 us (20%)
  matrix products  270 us (18%)
  between operations  198 us (13%)
    dot_general x1014, matrix products, matmul(): jnp.dot(left, right, precision=highest, preferred_element_type=jnp.float32)  228 us
    mul x255, other arithmetic, lower_upper(): working = working - multipliers[:, None] * working[column, :][None, :]  166 us
    slice x256, local copies, waits for them, and re-layouts, cholesky_pair(): pivot = jnp.sqrt(working[column, column])  150 us
    slice x256, local copies, waits for them, and re-layouts, lower_upper(): working[column, column]  148 us
    psum x2, waiting for transfers between devices, per_device(): products = lax.psum(transposed_product(reflectors, target), 'prow')  143 us
    psum x2, waiting for transfers between devices, factor_panel(): lax.psum((transposed_product(masked, masked), corner), 'prow')  109 us
    psum x1, waiting for transfers between devices, broadcast(): return lax.psum(jnp.where(mine, value, jnp.zeros_like(value)), axis)  52.6 us
    slice x255, local copies, waits for them, and re-layouts, lower_upper(): working = working - multipliers[:, None] * working[column, :][None, :]  44.5 us
  transfers between devices with their start and end apart: 5, of which 5 were waited for; matrix products, arithmetic and copies ran while one was open for 1% of the time, Pallas kernels for 0%

commit v1 on v0

v1 whole, which is shorter than its diff:
```python
import jax
import jax.numpy as jnp
from jax import lax
from jax.experimental import pallas as pl
from jax.experimental.pallas import tpu as pltpu
from jax.sharding import PartitionSpec as P

NB = 128
NP = 2 * NB

highest = lax.Precision.HIGHEST
high = lax.Precision.HIGH


def transposed_product(left, right, precision):
    return lax.dot_general(
        left, right, (((0,), (0,)), ((), ())), precision=precision, preferred_element_type=jnp.float32
    )


def matmul(left, right, precision=highest):
    return jnp.dot(left, right, precision=precision, preferred_element_type=jnp.float32)


def broadcast_first(value, axis, bits):
    size = lax.axis_size(axis)
    value = jnp.where(lax.axis_index(axis) == 0, value, 0.0)
    holders = [0]
    for bit in bits:
        pairs = [(i, i + bit) for i in holders if i + bit < size]
        value = value + lax.ppermute(value, axis, pairs)
        holders = holders + [target for _, target in pairs]
    return value


def identity_tile():
    rows = lax.broadcasted_iota(jnp.int32, (NB, NB), 0)
    cols = lax.broadcasted_iota(jnp.int32, (NB, NB), 1)
    return jnp.where(rows == cols, 1.0, 0.0)


def eliminate(systems):
    row_ids = lax.broadcasted_iota(jnp.int32, (NB, NB), 0)
    lane_ids = lax.broadcasted_iota(jnp.int32, (NB, NB), 1)
    for _, w_ref in systems:
        w_ref[...] = jnp.where(row_ids == lane_ids, 1.0, 0.0)

    def step(k, carry):
        for x_ref, w_ref in systems:
            x = x_ref[...]
            pivot_row = x_ref[pl.ds(k, 1), :]
            pivot_w = w_ref[pl.ds(k, 1), :]
            pick = lane_ids == k
            pivot = jnp.sum(jnp.where(pick[:1], pivot_row, 0.0), axis=1, keepdims=True)
            inverse = 1.0 / pivot
            column = jnp.sum(jnp.where(pick & (row_ids > k), x, 0.0), axis=1, keepdims=True)
            x_ref[...] = x - column * (pivot_row * inverse)
            w_ref[...] = w_ref[...] - column * (pivot_w * inverse)
        return carry

    lax.fori_loop(0, NB, step, 0)


def diagonal_column(x):
    return jnp.sum(x * identity_tile(), axis=1, keepdims=True)


def cholesky_kernel(gram_ref, upper_ref, inverse_ref, x_ref, w_ref):
    row_ids = lax.broadcasted_iota(jnp.int32, (NB, NB), 0)
    lane_ids = lax.broadcasted_iota(jnp.int32, (NB, NB), 1)
    lead, tail = pl.ds(0, NB), pl.ds(NB, NB)
    zero = jnp.zeros((NB, NB), jnp.float32)

    def block():
        eliminate([(x_ref, w_ref)])
        x = x_ref[...]
        scale = 1.0 / jnp.sqrt(diagonal_column(x))
        return jnp.where(row_ids <= lane_ids, x, 0.0) * scale, w_ref[...] * scale

    x_ref[...] = gram_ref[lead, lead]
    r00, i00 = block()
    upper_ref[lead, lead] = r00
    inverse_ref[lead, lead] = i00
    r01 = matmul(i00, gram_ref[lead, tail])
    upper_ref[lead, tail] = r01
    r01_t = r01.T
    x_ref[...] = gram_ref[tail, tail] - matmul(r01_t, r01)
    r11, i11 = block()
    upper_ref[tail, tail] = r11
    inverse_ref[tail, tail] = i11
    upper_ref[tail, lead] = zero
    inverse_ref[lead, tail] = zero
    inverse_ref[tail, lead] = -matmul(i11, matmul(r01_t, inverse_ref[lead, lead]))


def lower_upper_kernel(
    top_ref, upper_ref, inverse_ref, lower_ref, packed_ref, left_ref, right_ref, t_ref,
    s_ref, st_ref, li_ref, ui_ref, x_ref, w_ref, xt_ref, wt_ref,
):
    row_ids = lax.broadcasted_iota(jnp.int32, (NB, NB), 0)
    lane_ids = lax.broadcasted_iota(jnp.int32, (NB, NB), 1)
    lead, tail = pl.ds(0, NB), pl.ds(NB, NB)
    zero = jnp.zeros((NB, NB), jnp.float32)
    eye = identity_tile()
    s_ref[...] = matmul(top_ref[...], inverse_ref[...].T)
    s_ref[lead, lead] = s_ref[lead, lead] + eye
    s_ref[tail, tail] = s_ref[tail, tail] + eye
    st_ref[...] = s_ref[...].T

    def block(which, index):
        eliminate([(x_ref, w_ref), (xt_ref, wt_ref)])
        upper = jnp.where(row_ids <= lane_ids, x_ref[...], 0.0)
        xt = xt_ref[...]
        scale = 1.0 / diagonal_column(xt)
        lower_t = jnp.where(row_ids < lane_ids, xt * scale, eye)
        lower_ref[which, which] = lower_t.T
        li_ref[which, which] = w_ref[...]
        ui_ref[which, which] = wt_ref[...] * scale
        t_ref[index] = matmul(upper, w_ref[...].T)

    x_ref[...] = s_ref[lead, lead]
    xt_ref[...] = st_ref[lead, lead]
    block(lead, 0)
    u01 = matmul(li_ref[lead, lead], s_ref[lead, tail])
    l10_t = matmul(ui_ref[lead, lead], st_ref[lead, tail])
    l10, u01_t = l10_t.T, u01.T
    lower_ref[tail, lead] = l10
    lower_ref[lead, tail] = zero
    li_ref[lead, tail] = zero
    ui_ref[lead, tail] = zero
    li_ref[tail, lead] = matmul(l10, li_ref[lead, lead])
    ui_ref[tail, lead] = matmul(u01_t, ui_ref[lead, lead])
    corner = s_ref[tail, tail] - matmul(l10, u01)
    x_ref[...] = corner
    xt_ref[...] = corner.T
    block(tail, 1)
    li_ref[tail, lead] = -matmul(li_ref[tail, tail], li_ref[tail, lead])
    ui_ref[tail, lead] = -matmul(ui_ref[tail, tail], ui_ref[tail, lead])
    left_ref[...] = matmul(li_ref[...], inverse_ref[...])
    right_ref[...] = matmul(ui_ref[...], inverse_ref[...]).T
    all_rows = lax.broadcasted_iota(jnp.int32, (NP, NP), 0)
    all_lanes = lax.broadcasted_iota(jnp.int32, (NP, NP), 1)
    packed_ref[...] = jnp.where(all_rows <= all_lanes, -upper_ref[...], lower_ref[...])


def in_vmem(count):
    return [pl.BlockSpec(memory_space=pltpu.VMEM)] * count


def cholesky(gram):
    square = jax.ShapeDtypeStruct((NP, NP), jnp.float32)
    return pl.pallas_call(
        cholesky_kernel,
        name="cholesky",
        out_shape=(square, square),
        in_specs=in_vmem(1),
        out_specs=tuple(in_vmem(2)),
        scratch_shapes=[pltpu.VMEM((NB, NB), jnp.float32)] * 2,
        cost_estimate=pl.CostEstimate(flops=10**9, bytes_accessed=10**8, transcendentals=0),
    )(gram)


def lower_upper(top, upper, inverse):
    square = jax.ShapeDtypeStruct((NP, NP), jnp.float32)
    return pl.pallas_call(
        lower_upper_kernel,
        name="lower_upper",
        out_shape=(square,) * 4 + (jax.ShapeDtypeStruct((2, NB, NB), jnp.float32),),
        in_specs=in_vmem(3),
        out_specs=tuple(in_vmem(5)),
        scratch_shapes=[pltpu.VMEM((NP, NP), jnp.float32)] * 4
        + [pltpu.VMEM((NB, NB), jnp.float32)] * 4,
        cost_estimate=pl.CostEstimate(flops=10**9, bytes_accessed=10**8, transcendentals=0),
    )(top, upper, inverse)


def per_device(matrix):
    rows_dev = matrix.shape[0]
    my_row = lax.axis_index("prow")
    my_col = lax.axis_index("pcol")
    first = my_row == 0
    panel = matrix[:, :NP]
    gram_local = transposed_product(panel, panel, highest)
    top_local = jnp.where(first, panel[:NP], 0.0)
    both = jnp.where(my_col == 0, jnp.concatenate([gram_local, top_local], axis=0), 0.0)
    both = lax.psum(both, ("prow", "pcol"))
    bits = []
    while 2 ** len(bits) < lax.axis_size("pcol"):
        bits.append(2 ** len(bits))
    half = rows_dev // 2
    panel = jnp.concatenate(
        [
            broadcast_first(panel[:half], "pcol", bits),
            broadcast_first(panel[half:], "pcol", bits[::-1]),
        ],
        axis=0,
    )
    upper, inverse = cholesky(both[:NP])
    shifted = panel.at[:NP].add(jnp.where(first, upper, 0.0))
    products = lax.psum(transposed_product(shifted, matrix, high), "prow")
    lower, packed_top, left, right, tfactors = lower_upper(both[NP:], upper, inverse)
    reflectors = matmul(shifted, right)
    packed = reflectors.at[:NP].set(jnp.where(first, packed_top, reflectors[:NP]))
    reflectors = reflectors.at[:NP].set(jnp.where(first, lower, reflectors[:NP]))
    weights = matmul(left, products, high)
    result = matrix - matmul(reflectors, weights, high)
    result = result.at[:, :NP].set(jnp.where(my_col == 0, packed, result[:, :NP]))
    return (result, tfactors)


def solution(mesh):
    return jax.shard_map(
        per_device,
        mesh=mesh,
        in_specs=(P("prow", "pcol"),),
        out_specs=(P("prow", "pcol"), P()),
        check_vma=False,
    )
```

time: 1470 us -> 377 us (0.26)
  local copies, waits for them, and re-layouts: 395 us -> 1.92 us
  other arithmetic: 287 us -> 10 us
  matrix products: 270 us -> 57.9 us
  between operations: 198 us -> 14.2 us
  waiting for transfers between devices: 305 us -> 219 us
  Pallas kernels: 0 us -> 62 us
    slice x770 -> x1, local copies, waits for them, and re-layouts: 345 us -> 1.85 us  [per_device(): both[NP:]]
    dot_general x1018 -> x5, matrix products: 270 us -> 57.9 us  [the longest x3 36.2 us: matmul(): jnp.dot(left, right, precision=precision, preferred_element_type=jnp.floa...]
    mul x256 -> x0, other arithmetic: 166 us -> none  [the longest x255 166 us: lower_upper(): working = working - multipliers[:, None] * working[column, :][None, :]]
    psum x5 -> x2, waiting for transfers between devices: 305 us -> 214 us  [the longest x1 118 us: per_device(): both = lax.psum(both, ('prow', 'pcol'))]
    pallas_call x0 -> x2, Pallas kernels: none -> 62 us  [the longest x1 33.8 us: lower_upper(): pl.pallas_call(lower_upper_kernel, name='lower_upper', out_shape=(square,...]
    select_n x457 -> x3, other arithmetic: 51.5 us -> 3.08 us  [the longest x1 1.28 us: broadcast_first(): value = jnp.where(lax.axis_index(axis) == 0, value, 0.0)]
    sub x480 -> x0, other arithmetic: 47.7 us -> none  [the longest x224 27 us: cholesky_pair(): working = working - column_values[:, None] * column_values[None, :]]
    gather x64 -> x0, local copies, waits for them, and re-layouts: 40.5 us -> none  [the longest x32 20.3 us: cholesky_pair(): diagonal_values = jnp.diagonal(lower_part)]
  transfers between devices with their start and end apart: 5 -> 6, of which waited for: 5 -> 4; matrix products, arithmetic and copies ran while one was open for 1% -> 3% of each run, Pallas kernels for 0% -> 16%
where the time goes in v1:
time: 377 us; the launch traced here: 376 us
  waiting for transfers between devices  219 us (58%)
  Pallas kernels  62 us (16%)
  matrix products  57.9 us (15%)
  between operations  14.2 us (4%)
  starting transfers between devices  11.1 us (3%)
  other arithmetic  10 us (3%)
    psum x1, waiting for transfers between devices, per_device(): both = lax.psum(both, ('prow', 'pcol'))  118 us
    psum x1, waiting for transfers between devices, per_device(): products = lax.psum(transposed_product(shifted, matrix, high), 'prow')  95.7 us
    dot_general x3, matrix products, matmul(): jnp.dot(left, right, precision=precision, preferred_element_type=jnp.floa...  36.2 us
    pallas_call x1, Pallas kernels, lower_upper(): pl.pallas_call(lower_upper_kernel, name='lower_upper', out_shape=(square,...  33.8 us
    pallas_call x1, Pallas kernels, cholesky(): pl.pallas_call(cholesky_kernel, name='cholesky', out_shape=(square, squar...  28.2 us
    dot_general x2, matrix products, transposed_product(): lax.dot_general(left, right, (((0,), (0,)), ((), ())), precision=precisio...  21.7 us
    ppermute x4, starting transfers between devices, broadcast_first(): value = value + lax.ppermute(value, axis, pairs)  11 us
  transfers between devices with their start and end apart: 6, of which 4 were waited for; matrix products, arithmetic and copies ran while one was open for 3% of the time, Pallas kernels for 16%

profile of v1, /device:TPU:0, one launch (start us, length us, event | category | flops | bytes accessed | tf_op | source)
XLA Modules:
  0.0 376.4 jit_solution(17775592796841454501)
XLA Ops:
  7.2 0.0 all-reduce.3.cloned.1.call-start
  7.2 1.3 slice_select_fusion.1
  8.5 4.9 %collective-permute-start = (f32[512,256]{1,0:T(8,128)S(1)}, f32[512,256]{1,0:T(8,128)S(1)}, u32[]{:S(2)}, u32[]{:S(2)}) collective-permute-start(f32[512,256]{1,0:T(8,128)S(1)} %get-tuple-element.64), channel_id=1, source_target_pairs={{0,1},{4,5},{8,9},{12,13},{16,17},{20,21},{24,25},{28,29}} | collective-permute-start | bytes 1572872 | tf_op jit(solution)/shard_map/ppermute | solution.py:31
  13.4 1.3 collective-permute-start.2
  14.7 1.0 slice_select_fusion.2
  15.7 3.5 fusion.1
  19.2 0.8 maximum_select_fusion
  20.1 0.0 all-reduce.3.cloned.1.call-update
  20.1 0.0 all-reduce.5.cloned.1.call-start
  20.1 4.4 %collective-permute-done = f32[512,256]{1,0:T(8,128)S(1)} collective-permute-done((f32[512,256]{1,0:T(8,128)S(1)}, f32[512,256]{1,0:T(8,128)S(1)}, u32[]{:S(2)}, u32[]{:S(2)}) %collective-permute-start) | collective-permute-done | bytes 524320 | tf_op jit(solution)/shard_map/ppermute | solution.py:31
  24.5 0.1 add.29
  24.6 1.3 collective-permute-start.1
  25.9 1.2 collective-permute-done.2
  27.1 0.1 add.31
  27.2 3.4 collective-permute-start.3
  30.6 118.0 %all-reduce.3.cloned.1.call-done = f32[512,256]{1,0:T(8,128)} async-done(((f32[512,256]{1,0:T(8,128)}), f32[512,256]{1,0:T(8,128)}) %all-reduce.3.cloned.1.call-update) | async-done | bytes 524304 | tf_op jit(solution)/shard_map/psum | solution.py:186
  148.7 1.9 fusion.4
  150.5 28.2 %cholesky.1 = (f32[256,256]{1,0:T(8,128)}, f32[256,256]{1,0:T(8,128)}) custom-call(f32[256,256]{1,0:T(8,128)} %get-tuple-element.67.gram_ref), custom_call_target="tpu_custom_call" | custom-call | flops 1000000000 | bytes 100000000 | tf_op jit(solution)/shard_map/cholesky/pallas_call | solution.py:152
  178.7 0.0 collective-permute-done.1
  178.7 0.1 add.30
  178.8 0.0 collective-permute-done.3
  178.8 0.1 add.32
  178.9 0.1 pad_maximum_fusion
  178.9 1.0 fusion.3
  179.9 18.2 %fusion.6 = f32[256,6144]{1,0:T(8,128)} fusion(f32[1024,256]{1,0:T(8,128)S(1)} %fusion.3, f32[1024,6144]{1,0:T(8,128)} %param.9), kind=kOutput, calls=%fused_computation.17 | convolution fusion | flops 9663676416 | bytes 32505856 | tf_op jit(solution)/shard_map/dot_general | solution.py:16
  198.1 0.0 all-reduce.5.cloned.1.call-update
  198.1 0.6 compare_reduce_fusion
  198.8 33.8 %lower_upper.1 = (f32[256,256]{1,0:T(8,128)}, f32[256,256]{1,0:T(8,128)}, f32[256,256]{1,0:T(8,128)}, f32[256,256]{1,0:T(8,128)}, f32[2,128,128]{2,1,0:T(8,128)}) custom-call(f32[256,256]{1,0:T(8,128)} %get-tuple-element.66.top_ref, f32[256,256]{1,0:T(8,128)} %get-tuple-element.57.upper_ref, f32[256,256]{1,0:T(8,128)} %get-tuple-element.58.inverse_ref), custom_call_target="tpu_custom_call" | custom-call | flops 1000000000 | bytes 100000000 | tf_op jit(solution)/shard_map/lower_upper/pallas_call | solution.py:165
  232.6 1.9 fusion.5
  234.6 0.1 copy.7
  234.6 1.0 select_dynamic-update-slice_fusion.1
  235.7 1.0 select_dynamic-update-slice_fusion
  236.7 95.7 %all-reduce.5.cloned.1.call-done = f32[256,6144]{1,0:T(8,128)} async-done(((f32[256,6144]{1,0:T(8,128)}), f32[256,6144]{1,0:T(8,128)}) %all-reduce.5.cloned.1.call-update) | async-done | bytes 6291472 | tf_op jit(solution)/shard_map/psum | solution.py:200
  332.4 8.6 %fusion.7 = f32[256,6144]{1,0:T(8,128)} fusion(f32[256,256]{1,0:T(8,128)} %get-tuple-element.61, f32[256,6144]{1,0:T(8,128)} %all-reduce.5.cloned.1.call-done), kind=kOutput, calls=%fused_computation.18 | convolution fusion | flops 2415919104 | bytes 12845056 | tf_op jit(solution)/shard_map/dot_general | solution.py:22
  341.0 25.7 %convolution_subtract_fusion = f32[1024,6144]{1,0:T(8,128)} fusion(f32[1024,6144]{1,0:T(8,128)} %param.9, f32[1024,256]{1,0:T(8,128)S(1)} %select_dynamic-update-slice_fusion.1, f32[256,6144]{1,0:T(8,128)} %fusion.7), kind=kOutput, calls=%fused_computation | convolution fusion | flops 9669967872 | bytes 57671680 | tf_op jit(solution)/shard_map/dot_general | solution.py:22
  366.7 2.9 fusion
Async XLA Ops:
  7.2 141.5 %all-reduce.3.cloned.1.call-start = ((), (), s32[]{:S(2)}) async-start(), calls=%async_computation | async-start | bytes 1048576 | tf_op jit(solution)/shard_map/psum | solution.py:186
  8.5 16.0 %collective-permute-start = (f32[512,256]{1,0:T(8,128)S(1)}, f32[512,256]{1,0:T(8,128)S(1)}, u32[]{:S(2)}, u32[]{:S(2)}) collective-permute-start(f32[512,256]{1,0:T(8,128)S(1)} %get-tuple-element.64), channel_id=1, source_target_pairs={{0,1},{4,5},{8,9},{12,13},{16,17},{20,21},{24,25},{28,29}} | collective-permute-start | bytes 1572872 | tf_op jit(solution)/shard_map/ppermute | solution.py:31
  13.4 13.7 %collective-permute-start.2 = (f32[512,256]{1,0:T(8,128)S(1)}, f32[512,256]{1,0:T(8,128)S(1)}, u32[]{:S(2)}, u32[]{:S(2)}) collective-permute-start(f32[512,256]{1,0:T(8,128)S(1)} %get-tuple-element.65), channel_id=1, source_target_pairs={{0,2},{4,6},{8,10},{12,14},{16,18},{20,22},{24,26},{28,30}} | collective-permute-start | bytes 1572872 | tf_op jit(solution)/shard_map/ppermute | solution.py:31
  20.1 312.3 %all-reduce.5.cloned.1.call-start = ((), (), s32[]{:S(2)}) async-start(), calls=%async_computation.1 | async-start | bytes 12582912 | tf_op jit(solution)/shard_map/psum | solution.py:200
  24.6 154.1 %collective-permute-start.1 = (f32[512,256]{1,0:T(8,128)S(1)}, f32[512,256]{1,0:T(8,128)S(1)}, u32[]{:S(2)}, u32[]{:S(2)}) collective-permute-start(f32[512,256]{1,0:T(8,128)S(1)} %add.29), channel_id=1, source_target_pairs={{0,2},{1,3},{4,6},{5,7},{8,10},{9,11},{12,14},{13,15},{16,18},{17,... | collective-permute-start | bytes 1572872 | tf_op jit(solution)/shard_map/ppermute | solution.py:31
  27.2 151.6 %collective-permute-start.3 = (f32[512,256]{1,0:T(8,128)S(1)}, f32[512,256]{1,0:T(8,128)S(1)}, u32[]{:S(2)}, u32[]{:S(2)}) collective-permute-start(f32[512,256]{1,0:T(8,128)S(1)} %add.31), channel_id=1, source_target_pairs={{0,1},{2,3},{4,5},{6,7},{8,9},{10,11},{12,13},{14,15},{16,17},{18,... | collective-permute-start | bytes 1572872 | tf_op jit(solution)/shard_map/ppermute | solution.py:31
Sparse Core Ops, SparseCore 0:
  20.2 128.3 all-reduce.2
  198.2 134.1 all-reduce.4

commit v2 on v1

--- a/solution.py
+++ b/solution.py
@@ -30,6 +30,22 @@
         pairs = [(i, i + bit) for i in holders if i + bit < size]
         value = value + lax.ppermute(value, axis, pairs)
         holders = holders + [target for _, target in pairs]
+    return value
+
+
+def doublings(axis):
+    bits = []
+    while 2 ** len(bits) < lax.axis_size(axis):
+        bits.append(2 ** len(bits))
+    return bits
+
+
+def butterfly_sum(value, axis):
+    size = lax.axis_size(axis)
+    if size & (size - 1):
+        return lax.psum(value, axis)
+    for bit in doublings(axis):
+        value = value + lax.ppermute(value, axis, [(i, i ^ bit) for i in range(size)])
     return value
 
 
@@ -180,13 +196,7 @@
     my_col = lax.axis_index("pcol")
     first = my_row == 0
     panel = matrix[:, :NP]
-    gram_local = transposed_product(panel, panel, highest)
-    top_local = jnp.where(first, panel[:NP], 0.0)
-    both = jnp.where(my_col == 0, jnp.concatenate([gram_local, top_local], axis=0), 0.0)
-    both = lax.psum(both, ("prow", "pcol"))
-    bits = []
-    while 2 ** len(bits) < lax.axis_size("pcol"):
-        bits.append(2 ** len(bits))
+    bits = doublings("pcol")
     half = rows_dev // 2
     panel = jnp.concatenate(
         [
@@ -195,10 +205,12 @@
         ],
         axis=0,
     )
-    upper, inverse = cholesky(both[:NP])
+    gram = butterfly_sum(transposed_product(panel, panel, highest), "prow")
+    top = broadcast_first(panel[:NP], "prow", doublings("prow")[::-1])
+    upper, inverse = cholesky(gram)
     shifted = panel.at[:NP].add(jnp.where(first, upper, 0.0))
     products = lax.psum(transposed_product(shifted, matrix, high), "prow")
-    lower, packed_top, left, right, tfactors = lower_upper(both[NP:], upper, inverse)
+    lower, packed_top, left, right, tfactors = lower_upper(top, upper, inverse)
     reflectors = matmul(shifted, right)
     packed = reflectors.at[:NP].set(jnp.where(first, packed_top, reflectors[:NP]))
     reflectors = reflectors.at[:NP].set(jnp.where(first, lower, reflectors[:NP]))

time: 377 us -> 299 us (0.79)
  waiting for transfers between devices: 219 us -> 136 us
  starting transfers between devices: 11.1 us -> 20 us
    psum x1 -> x0, waiting for transfers between devices: 118 us -> none  [per_device(): both = lax.psum(both, ('prow', 'pcol'))]
    ppermute x4 -> x7, waiting for transfers between devices: 5.59 us -> 34.3 us  [broadcast_first(): value = value + lax.ppermute(value, axis, pairs)]
    ppermute x0 -> x3, waiting for transfers between devices: none -> 19.6 us  [butterfly_sum(): lax.ppermute(value, axis, [(i, i ^ bit) for i in range(size)])]
    psum x1, waiting for transfers between devices: 95.7 us -> 81.9 us  [per_device(): products = lax.psum(transposed_product(shifted, matrix, high), 'prow')]
    ppermute x4 -> x7, starting transfers between devices: 11 us -> 15.5 us  [broadcast_first(): value = value + lax.ppermute(value, axis, pairs)]
    ppermute x0 -> x3, starting transfers between devices: none -> 4.37 us  [butterfly_sum(): lax.ppermute(value, axis, [(i, i ^ bit) for i in range(size)])]
  transfers between devices with their start and end apart: 6 -> 11, of which waited for: 4 -> 11; matrix products, arithmetic and copies ran while one was open for 3% -> 2% of each run, Pallas kernels for 16% -> 11%
where the time goes in v2:
time: 299 us; the launch traced here: 298 us
  waiting for transfers between devices  136 us (45%)
  Pallas kernels  62.1 us (21%)
  matrix products  56.2 us (19%)
  starting transfers between devices  20 us (7%)
  between operations  14.2 us (5%)
  other arithmetic  9.77 us (3%)
    psum x1, waiting for transfers between devices, per_device(): products = lax.psum(transposed_product(shifted, matrix, high), 'prow')  81.9 us
    dot_general x3, matrix products, matmul(): jnp.dot(left, right, precision=precision, preferred_element_type=jnp.floa...  36.2 us
    ppermute x7, waiting for transfers between devices, broadcast_first(): value = value + lax.ppermute(value, axis, pairs)  34.3 us
    pallas_call x1, Pallas kernels, lower_upper(): pl.pallas_call(lower_upper_kernel, name='lower_upper', out_shape=(square,...  33.9 us
    pallas_call x1, Pallas kernels, cholesky(): pl.pallas_call(cholesky_kernel, name='cholesky', out_shape=(square, squar...  28.2 us
    dot_general x2, matrix products, transposed_product(): lax.dot_general(left, right, (((0,), (0,)), ((), ())), precision=precisio...  20 us
    ppermute x3, waiting for transfers between devices, butterfly_sum(): lax.ppermute(value, axis, [(i, i ^ bit) for i in range(size)])  19.6 us
    ppermute x7, starting transfers between devices, broadcast_first(): value = value + lax.ppermute(value, axis, pairs)  15.5 us
  transfers between devices with their start and end apart: 11, of which 11 were waited for; matrix products, arithmetic and copies ran while one was open for 2% of the time, Pallas kernels for 11%

profile of v2, /device:TPU:0, one launch (start us, length us, event | category | flops | bytes accessed | tf_op | source)
XLA Modules:
  0.0 298.1 jit_solution(15980645872531148455)
XLA Ops:
  7.2 0.0 all-reduce.2.cloned.1.call-start
  7.2 1.3 slice_select_fusion.1
  8.5 4.9 %collective-permute-start = (f32[512,256]{1,0:T(8,128)S(1)}, f32[512,256]{1,0:T(8,128)S(1)}, u32[]{:S(2)}, u32[]{:S(2)}) collective-permute-start(f32[512,256]{1,0:T(8,128)S(1)} %get-tuple-element.64), channel_id=1, source_target_pairs={{0,1},{4,5},{8,9},{12,13},{16,17},{20,21},{24,25},{28,29}} | collective-permute-start | bytes 1572872 | tf_op jit(solution)/shard_map/ppermute | solution.py:31
  13.4 1.3 collective-permute-start.2
  14.7 9.8 %collective-permute-done = f32[512,256]{1,0:T(8,128)S(1)} collective-permute-done((f32[512,256]{1,0:T(8,128)S(1)}, f32[512,256]{1,0:T(8,128)S(1)}, u32[]{:S(2)}, u32[]{:S(2)}) %collective-permute-start) | collective-permute-done | bytes 524320 | tf_op jit(solution)/shard_map/ppermute | solution.py:31
  24.5 0.1 add.45
  24.6 1.3 collective-permute-start.1
  25.9 0.5 collective-permute-done.2
  26.5 0.1 add.47
  26.5 3.9 %collective-permute-start.3 = (f32[512,256]{1,0:T(8,128)S(1)}, f32[512,256]{1,0:T(8,128)S(1)}, u32[]{:S(2)}, u32[]{:S(2)}) collective-permute-start(f32[512,256]{1,0:T(8,128)S(1)} %add.47), channel_id=1, source_target_pairs={{0,1},{2,3},{4,5},{6,7},{8,9},{10,11},{12,13},{14,15},{16,17},{18,... | collective-permute-start | bytes 1572872 | tf_op jit(solution)/shard_map/ppermute | solution.py:31
  30.5 6.6 %collective-permute-done.1 = f32[512,256]{1,0:T(8,128)S(1)} collective-permute-done((f32[512,256]{1,0:T(8,128)S(1)}, f32[512,256]{1,0:T(8,128)S(1)}, u32[]{:S(2)}, u32[]{:S(2)}) %collective-permute-start.1) | collective-permute-done | bytes 524320 | tf_op jit(solution)/shard_map/ppermute | solution.py:31
  37.1 0.1 add.46
  37.2 3.6 %collective-permute-done.3 = f32[512,256]{1,0:T(8,128)S(1)} collective-permute-done((f32[512,256]{1,0:T(8,128)S(1)}, f32[512,256]{1,0:T(8,128)S(1)}, u32[]{:S(2)}, u32[]{:S(2)}) %collective-permute-start.3) | collective-permute-done | bytes 524320 | tf_op jit(solution)/shard_map/ppermute | solution.py:31
  40.7 0.1 add.48
  40.8 1.8 fusion.1
  42.6 0.1 collective-permute-start.4
  42.7 1.5 collective-permute-done.4
  44.3 1.6 collective-permute-start.5
  45.9 6.8 %collective-permute-done.5 = f32[256,256]{1,0:T(8,128)S(1)} collective-permute-done((f32[256,256]{1,0:T(8,128)S(1)}, f32[256,256]{1,0:T(8,128)S(1)}, u32[]{:S(2)}, u32[]{:S(2)}) %collective-permute-start.5) | collective-permute-done | bytes 262176 | tf_op jit(solution)/shard_map/ppermute | solution.py:48
  52.7 2.7 collective-permute-start.6
  55.4 0.1 pad_maximum_fusion
  55.5 11.3 %collective-permute-done.6 = f32[256,256]{1,0:T(8,128)S(1)} collective-permute-done((f32[256,256]{1,0:T(8,128)S(1)}, f32[256,256]{1,0:T(8,128)S(1)}, u32[]{:S(2)}, u32[]{:S(2)}) %collective-permute-start.6) | collective-permute-done | bytes 262176 | tf_op jit(solution)/shard_map/ppermute | solution.py:48
  66.8 0.7 add.51.gram_ref
  67.6 28.2 %cholesky.1 = (f32[256,256]{1,0:T(8,128)}, f32[256,256]{1,0:T(8,128)}) custom-call(f32[256,256]{1,0:T(8,128)} %add.51.gram_ref), custom_call_target="tpu_custom_call" | custom-call | flops 1000000000 | bytes 100000000 | tf_op jit(solution)/shard_map/cholesky/pallas_call | solution.py:168
  95.7 1.0 slice_select_fusion.2
  96.7 18.2 %fusion.3 = f32[256,6144]{1,0:T(8,128)} fusion(f32[1024,256]{1,0:T(8,128)S(1)} %get-tuple-element.67, f32[1024,6144]{1,0:T(8,128)} %param.9), kind=kOutput, calls=%fused_computation.13 | convolution fusion | flops 9663676416 | bytes 32505856 | tf_op jit(solution)/shard_map/dot_general | solution.py:16
  114.9 0.0 all-reduce.2.cloned.1.call-update
  114.9 1.3 collective-permute-start.7
  116.2 3.9 %collective-permute-done.7 = f32[256,256]{1,0:T(8,128)S(1)} collective-permute-done((f32[256,256]{1,0:T(8,128)S(1)}, f32[256,256]{1,0:T(8,128)S(1)}, u32[]{:S(2)}, u32[]{:S(2)}) %collective-permute-start.7) | collective-permute-done | bytes 262176 | tf_op jit(solution)/shard_map/ppermute | solution.py:31
  120.1 1.3 collective-permute-start.8
  121.4 9.6 %collective-permute-done.8 = f32[256,256]{1,0:T(8,128)S(1)} collective-permute-done((f32[256,256]{1,0:T(8,128)S(1)}, f32[256,256]{1,0:T(8,128)S(1)}, u32[]{:S(2)}, u32[]{:S(2)}) %collective-permute-start.8) | collective-permute-done | bytes 262176 | tf_op jit(solution)/shard_map/ppermute | solution.py:31
  131.1 1.5 collective-permute-start.9
  132.6 0.6 compare_reduce_fusion
  133.2 0.3 collective-permute-done.9
  133.5 0.7 add.55.top_ref
  134.3 33.9 %lower_upper.1 = (f32[256,256]{1,0:T(8,128)}, f32[256,256]{1,0:T(8,128)}, f32[256,256]{1,0:T(8,128)}, f32[256,256]{1,0:T(8,128)}, f32[2,128,128]{2,1,0:T(8,128)}) custom-call(f32[256,256]{1,0:T(8,128)} %add.55.top_ref, f32[256,256]{1,0:T(8,128)} %get-tuple-element.57.upper_ref, f32[256,256]{1,0:T(8,128)} %get-tuple-element.58.inverse_ref), custom_call_target="tpu_custom_call" | custom-call | flops 1000000000 | bytes 100000000 | tf_op jit(solution)/shard_map/lower_upper/pallas_call | solution.py:181
  168.1 1.9 fusion.2
  170.1 0.1 copy.6
  170.1 1.0 select_dynamic-update-slice_fusion.1
  171.2 1.0 select_dynamic-update-slice_fusion
  172.2 81.9 %all-reduce.2.cloned.1.call-done = f32[256,6144]{1,0:T(8,128)} async-done(((f32[256,6144]{1,0:T(8,128)}), f32[256,6144]{1,0:T(8,128)}) %all-reduce.2.cloned.1.call-update) | async-done | bytes 6291472 | tf_op jit(solution)/shard_map/psum | solution.py:212
  254.1 8.6 %fusion.4 = f32[256,6144]{1,0:T(8,128)} fusion(f32[256,256]{1,0:T(8,128)} %get-tuple-element.61, f32[256,6144]{1,0:T(8,128)} %all-reduce.2.cloned.1.call-done), kind=kOutput, calls=%fused_computation.14 | convolution fusion | flops 2415919104 | bytes 12845056 | tf_op jit(solution)/shard_map/dot_general | solution.py:22
  262.7 25.7 %convolution_subtract_fusion = f32[1024,6144]{1,0:T(8,128)} fusion(f32[1024,6144]{1,0:T(8,128)} %param.9, f32[1024,256]{1,0:T(8,128)S(1)} %select_dynamic-update-slice_fusion.1, f32[256,6144]{1,0:T(8,128)} %fusion.4), kind=kOutput, calls=%fused_computation | convolution fusion | flops 9669967872 | bytes 57671680 | tf_op jit(solution)/shard_map/dot_general | solution.py:22
  288.4 2.9 fusion
  (4 shorter events, 0.1 us)
Async XLA Ops:
  7.2 246.9 %all-reduce.2.cloned.1.call-start = ((), (), s32[]{:S(2)}) async-start(), calls=%async_computation | async-start | bytes 12582912 | tf_op jit(solution)/shard_map/psum | solution.py:212
  8.5 16.0 %collective-permute-start = (f32[512,256]{1,0:T(8,128)S(1)}, f32[512,256]{1,0:T(8,128)S(1)}, u32[]{:S(2)}, u32[]{:S(2)}) collective-permute-start(f32[512,256]{1,0:T(8,128)S(1)} %get-tuple-element.64), channel_id=1, source_target_pairs={{0,1},{4,5},{8,9},{12,13},{16,17},{20,21},{24,25},{28,29}} | collective-permute-start | bytes 1572872 | tf_op jit(solution)/shard_map/ppermute | solution.py:31
  13.4 13.1 %collective-permute-start.2 = (f32[512,256]{1,0:T(8,128)S(1)}, f32[512,256]{1,0:T(8,128)S(1)}, u32[]{:S(2)}, u32[]{:S(2)}) collective-permute-start(f32[512,256]{1,0:T(8,128)S(1)} %get-tuple-element.65), channel_id=1, source_target_pairs={{0,2},{4,6},{8,10},{12,14},{16,18},{20,22},{24,26},{28,30}} | collective-permute-start | bytes 1572872 | tf_op jit(solution)/shard_map/ppermute | solution.py:31
  24.6 12.5 %collective-permute-start.1 = (f32[512,256]{1,0:T(8,128)S(1)}, f32[512,256]{1,0:T(8,128)S(1)}, u32[]{:S(2)}, u32[]{:S(2)}) collective-permute-start(f32[512,256]{1,0:T(8,128)S(1)} %add.45), channel_id=1, source_target_pairs={{0,2},{1,3},{4,6},{5,7},{8,10},{9,11},{12,14},{13,15},{16,18},{17,... | collective-permute-start | bytes 1572872 | tf_op jit(solution)/shard_map/ppermute | solution.py:31
  26.5 14.2 %collective-permute-start.3 = (f32[512,256]{1,0:T(8,128)S(1)}, f32[512,256]{1,0:T(8,128)S(1)}, u32[]{:S(2)}, u32[]{:S(2)}) collective-permute-start(f32[512,256]{1,0:T(8,128)S(1)} %add.47), channel_id=1, source_target_pairs={{0,1},{2,3},{4,5},{6,7},{8,9},{10,11},{12,13},{14,15},{16,17},{18,... | collective-permute-start | bytes 1572872 | tf_op jit(solution)/shard_map/ppermute | solution.py:31
  42.6 1.6 collective-permute-start.4
  44.3 8.4 %collective-permute-start.5 = (f32[256,256]{1,0:T(8,128)S(1)}, f32[256,256]{1,0:T(8,128)S(1)}, u32[]{:S(2)}, u32[]{:S(2)}) collective-permute-start(f32[256,256]{1,0:T(8,128)S(1)} %add.49), channel_id=1, source_target_pairs={{0,8},{4,12},{8,0},{12,4},{16,24},{20,28},{24,16},{28,20},{1,9},{5... | collective-permute-start | bytes 786440 | tf_op jit(solution)/shard_map/ppermute | solution.py:48
  52.7 14.1 %collective-permute-start.6 = (f32[256,256]{1,0:T(8,128)S(1)}, f32[256,256]{1,0:T(8,128)S(1)}, u32[]{:S(2)}, u32[]{:S(2)}) collective-permute-start(f32[256,256]{1,0:T(8,128)S(1)} %add.50), channel_id=1, source_target_pairs={{0,16},{4,20},{8,24},{12,28},{16,0},{20,4},{24,8},{28,12},{1,17},{... | collective-permute-start | bytes 786440 | tf_op jit(solution)/shard_map/ppermute | solution.py:48
  114.9 5.2 %collective-permute-start.7 = (f32[256,256]{1,0:T(8,128)S(1)}, f32[256,256]{1,0:T(8,128)S(1)}, u32[]{:S(2)}, u32[]{:S(2)}) collective-permute-start(f32[256,256]{1,0:T(8,128)S(1)} %get-tuple-element.66), channel_id=1, source_target_pairs={{0,16},{1,17},{2,18},{3,19}} | collective-permute-start | bytes 786440 | tf_op jit(solution)/shard_map/ppermute | solution.py:31
  120.1 10.9 %collective-permute-start.8 = (f32[256,256]{1,0:T(8,128)S(1)}, f32[256,256]{1,0:T(8,128)S(1)}, u32[]{:S(2)}, u32[]{:S(2)}) collective-permute-start(f32[256,256]{1,0:T(8,128)S(1)} %add.53), channel_id=1, source_target_pairs={{0,8},{16,24},{1,9},{17,25},{2,10},{18,26},{3,11},{19,27}} | collective-permute-start | bytes 786440 | tf_op jit(solution)/shard_map/ppermute | solution.py:31
  131.1 2.4 collective-permute-start.9
Sparse Core Ops, SparseCore 0:
  115.0 139.0 all-reduce.1
